TPU v7x, 32 devices: a whole 2x2x4 slice. The times are simulated.
32 devices in a mesh: grp: 4 (over x, core), dev: 8 (over z, y).
Axes of the slice: x: 2, y: 2, z: 4, core: 2. Of those that a mesh axis runs over, the one named last changes fastest.
Arguments:
- points: bfloat16 [65536, 1024], P(('grp', 'dev')), may hold values from -6 to 6
- blocks: int32 [65536, 1], P(('grp', 'dev')), may hold values from 0 to 63; in each aligned block of 2048 rows (0 to 2047, 2048 to 4095, ...) at most 64 rows name the same one
- finals: int32 [65536], P(('grp', 'dev')), may hold values from 0 to 255
- centroids: bfloat16 [16384, 1024], P('dev'), may hold values from -6 to 6
Outputs:
- distances: bfloat16 [65536, 256], P(('grp', 'dev'))
- refreshed_centroids: float32 [16384, 1024], P('dev', 'grp')
Inputs may be any that keep to these rules, and one draw needn't show every extreme that they name: `blocks`: among the 2048 rows of one device no block is named by more than 64 rows, and some block by exactly 64. Block b is held by index b // 8 of dev. The point's centroid is row 256 * blocks + finals of centroids.
All inputs are finite; a program needn't handle non-finite values.
Results may differ from a plain program's by a relative error of at most 0.008.
Values may be sent and summed in bfloat16 or wider, within the bound.
A program may use at most 128 MiB of HBM per device.

v0:
```python
import jax
import jax.numpy as jnp
from jax import lax
from jax.sharding import PartitionSpec as P

BS = 256


def block_work(received_points, wanted, centroid_table, width, block_size):
    cent_norm = jnp.sum(jnp.square(centroid_table.astype(jnp.float32)), axis=-1)
    row_norm = jnp.sum(jnp.square(received_points.astype(jnp.float32)), axis=-1)
    cross_products = jnp.einsum(
        "nzy,nvy->nzv", received_points, centroid_table, preferred_element_type=jnp.float32
    )
    dists = ((row_norm[:, :, None] - 2.0 * cross_products + cent_norm[:, None, :]) / width).astype(
        jnp.bfloat16
    )
    onehot_assign = wanted[:, :, None] == jnp.arange(block_size, dtype=jnp.int32)[None, None, :]
    sums = jnp.einsum(
        "xnt,xni->xti",
        onehot_assign.astype(jnp.bfloat16),
        received_points,
        preferred_element_type=jnp.float32,
    )
    counts = jnp.sum(onehot_assign.astype(jnp.float32), axis=1)
    return (dists, sums, counts)


def shards(points, blocks, finals, centroids):
    shard_counts = lax.axis_size("dev")
    count_grp = lax.axis_size("grp")
    npoints, width = points.shape
    block_size = BS
    owned = centroids.shape[0] // block_size
    nblocks = owned * shard_counts
    depth = 2 * npoints // nblocks
    block_ids = blocks[:, 0]
    labels = jnp.arange(nblocks, dtype=jnp.int32)
    member = block_ids[:, None] == labels[None, :]
    lower = (jnp.arange(npoints)[:, None] > jnp.arange(npoints)[None, :]).astype(jnp.bfloat16)
    before = jnp.dot(lower, member.astype(jnp.bfloat16), preferred_element_type=jnp.float32)
    ranks = jnp.sum(jnp.where(member, before, 0.0), axis=1).astype(jnp.int32)
    share = width // count_grp
    slots = block_ids * depth + ranks
    outgoing = jnp.zeros((nblocks * depth, width), jnp.bfloat16).at[slots].set(points)
    targets = jnp.full((nblocks * depth,), -1, jnp.int32).at[slots].set(finals)
    outgoing = outgoing.reshape(nblocks, depth, width)
    targets = targets.reshape(nblocks, depth)
    received_points, wanted = (
        lax.all_to_all(outgoing, "dev", split_axis=0, concat_axis=1, tiled=True),
        lax.all_to_all(targets, "dev", split_axis=0, concat_axis=1, tiled=True),
    )
    centroid_table = centroids.reshape(owned, block_size, width)
    dists, sums, counts = block_work(received_points, wanted, centroid_table, width, block_size)
    sums = sums.reshape(owned * block_size, width)
    counts = counts.reshape(owned * block_size)
    returned = lax.all_to_all(dists, "dev", split_axis=1, concat_axis=0, tiled=True)
    distances = returned.reshape(nblocks * depth, block_size)[slots]
    col_sums = lax.psum_scatter(
        sums.astype(jnp.bfloat16), "grp", scatter_dimension=1, tiled=True
    ).astype(jnp.float32)
    all_counts = lax.psum(counts, "grp")
    own_cols = lax.dynamic_slice_in_dim(centroids, lax.axis_index("grp") * share, share, 1).astype(
        jnp.float32
    )
    refreshed_centroids = (col_sums + own_cols) / (all_counts + 1.0)[:, None]
    return (distances, refreshed_centroids)


def solution(mesh):
    placed = (P(("grp", "dev"), None), P(("grp", "dev"), None), P(("grp", "dev")), P("dev", None))
    return jax.shard_map(
        shards,
        mesh=mesh,
        in_specs=placed,
        out_specs=(P(("grp", "dev"), None), P("dev", "grp")),
        check_vma=False,
    )
```

profile of v0, /device:TPU:0, one launch (start us, length us, event | category | flops | bytes accessed | tf_op | source)
XLA Modules:
  0.0 339.8 jit_solution(2973195217341700019)
XLA Ops:
  7.2 0.0 copy-start.1
  7.2 2.5 fusion.7
  9.6 0.0 copy-done.1
  9.7 8.2 %scatter_custom_fusion.1 = s32[4096]{0:T(1024)S(1)} fusion(s32[2048]{0:T(1024)S(1)} %bitcast.28, s32[2048]{0:T(1024)} %param.6, s32[]{:T(128)} %constant.8.clone.1), kind=kCustom, calls=%fused_computation.21 | custom fusion | bytes 16896 | tf_op jit(solution)/shard_map/scatter | solution.py:46
  17.9 0.1 all_to_all.43
  18.0 0.7 reshape.73
  18.7 7.3 %all-to-all-start.2 = ((s32[8,1,512]{2,1,0:T(1,128)}), s32[8,1,512]{2,1,0:T(1,128)S(1)}, u32[]{:S(2)}, u32[]{:S(2)}) async-start(s32[8,1,512]{2,1,0:T(1,128)} %reshape.73), calls=%async_computation.2 | async-start | bytes 32768 | tf_op jit(solution)/shard_map/all_to_all | solution.py:51
  26.0 15.2 %scatter_custom_fusion = bf16[4096,1024]{1,0:T(8,128)(2,1)} fusion(s32[2048]{0:T(1024)S(1)} %bitcast.29, bf16[2048,1024]{1,0:T(8,128)(2,1)} %param.4, bf16[]{:T(256)} %constant.12.clone.1), kind=kCustom, calls=%fused_computation.11 | custom fusion | bytes 8389120 | tf_op jit(solution)/shard_map/scatter | solution.py:45
  41.2 0.0 all-to-all-done.2
  41.2 6.0 %all-to-all-start = ((bf16[64,64,1024]{2,1,0:T(8,128)(2,1)}), bf16[64,64,1024]{2,1,0:T(8,128)(2,1)}, u32[]{:S(2)}, u32[]{:S(2)}) async-start(bf16[64,64,1024]{2,1,0:T(8,128)(2,1)} %bitcast.21), calls=%async_computation | async-start | bytes 16777216 | tf_op jit(solution)/shard_map/all_to_all | solution.py:50
  47.2 0.2 reduce-scatter.2.cloned.1.call-start
  47.5 0.5 broadcast.19
  48.0 0.7 reduce.2
  48.7 0.1 reshape.74
  48.8 0.1 eq.34
  48.8 181.0 %all-to-all-done = bf16[64,64,1024]{2,1,0:T(8,128)(2,1)} async-done(((bf16[64,64,1024]{2,1,0:T(8,128)(2,1)}), bf16[64,64,1024]{2,1,0:T(8,128)(2,1)}, u32[]{:S(2)}, u32[]{:S(2)}) %all-to-all-start) | async-done | bytes 8388640 | tf_op jit(solution)/shard_map/all_to_all | solution.py:50
  229.8 8.4 %copy.17 = bf16[8,8,64,1024]{3,2,1,0:T(8,128)(2,1)} copy(bf16[8,8,64,1024]{3,2,0,1:T(8,128)(2,1)} %bitcast.5) | data formatting | bytes 16777216 | tf_op jit(solution)/shard_map/all_to_all | solution.py:50
  238.2 7.7 %fusion.4 = bf16[8,256,1024]{2,1,0:T(8,128)(2,1)} fusion(bf16[8,512,1024]{2,1,0:T(8,128)(2,1)} %bitcast.22, s32[8,512]{1,0:T(8,128)S(1)} %eq.34), kind=kOutput, calls=%fused_computation.13 | convolution fusion | flops 2150629376 | bytes 12599296 | tf_op jit(solution)/shard_map/xnt,xni->xti/dot_general | solution.py:19
  245.9 0.0 reduce-scatter.2.cloned.1.call-update
  245.9 3.1 multiply_reduce_fusion.1
  249.0 6.0 %multiply_reduce_fusion = f32[8,8,64]{2,0,1:T(8,128)S(1)} fusion(bf16[8,8,64,1024]{3,2,0,1:T(8,128)(2,1)} %bitcast.5), kind=kLoop, calls=%fused_computation.3 | loop fusion | flops 12578816 | bytes 8404992 | tf_op jit(solution)/shard_map/reduce_sum | solution.py:11
  255.0 0.1 sub.10
  255.1 7.3 %multiply_convert_fusion = bf16[8,512,256]{2,1,0:T(8,128)(2,1)S(1)} fusion(bf16[8,512,1024]{2,1,0:T(8,128)(2,1)} %bitcast.23, bf16[8,256,1024]{2,1,0:T(8,128)(2,1)} %bitcast.25, f32[8,256]{1,0:T(8,128)S(1)} %add.38, f32[8,512]{1,0:T(8,128)S(1)} %sub.10), kind=kOutput, calls=%fused_computation.10 | convolution fusion | flops 2152726528 | bytes 14704640 | tf_op jit(solution)/shard_map/nzy,nvy->nzv/dot_general | solution.py:12
  262.4 2.5 copy.18
  264.9 3.9 %all-to-all-start.1 = ((bf16[8,512,256]{2,0,1:T(8,128)(2,1)}), bf16[8,512,256]{2,0,1:T(8,128)(2,1)S(1)}, u32[]{:S(2)}, u32[]{:S(2)}) async-start(bf16[8,512,256]{2,0,1:T(8,128)(2,1)} %copy.18), calls=%async_computation.1 | async-start | bytes 4194304 | tf_op jit(solution)/shard_map/all_to_all | solution.py:57
  268.8 0.5 convert_reduce_fusion
  269.3 7.7 %psum.7 = f32[2048]{0:T(1024)S(1)} all-reduce(f32[2048]{0:T(1024)S(1)} %bitcast.33), channel_id=1, replica_groups=mesh['grp'=4,'dev'=8] {'grp'}, use_global_device_ids=true, to_apply=%region_7.8 | all-reduce | flops 2048 | bytes 16384 | tf_op jit(solution)/shard_map/psum | solution.py:62
  277.1 40.2 %all-to-all-done.1 = bf16[8,512,256]{2,0,1:T(8,128)(2,1)S(1)} async-done(((bf16[8,512,256]{2,0,1:T(8,128)(2,1)}), bf16[8,512,256]{2,0,1:T(8,128)(2,1)S(1)}, u32[]{:S(2)}, u32[]{:S(2)}) %all-to-all-start.1) | async-done | bytes 2097184 | tf_op jit(solution)/shard_map/all_to_all | solution.py:57
  317.3 0.0 copy-start
  317.3 1.3 copy-done
  318.6 2.1 copy.19
  320.7 9.1 %gather_fusion = bf16[2048,256]{1,0:T(8,128)(2,1)} fusion(bf16[4096,256]{1,0:T(8,128)(2,1)S(1)} %bitcast.20, s32[2048]{0:T(1024)S(1)} %broadcast_clamp_fusion), kind=kCustom, calls=%fused_computation | custom fusion | bytes 2105344 | tf_op jit(solution)/shard_map/gather | solution.py:58
  329.8 0.0 reduce-scatter.2.cloned.1.call-done
  329.8 3.2 add_divide_fusion
  (8 shorter events, 0.1 us)
Async XLA Ops:
  7.2 2.5 copy-start.1
  18.7 22.6 %all-to-all-start.2 = ((s32[8,1,512]{2,1,0:T(1,128)}), s32[8,1,512]{2,1,0:T(1,128)S(1)}, u32[]{:S(2)}, u32[]{:S(2)}) async-start(s32[8,1,512]{2,1,0:T(1,128)} %reshape.73), calls=%async_computation.2 | async-start | bytes 32768 | tf_op jit(solution)/shard_map/all_to_all | solution.py:51
  41.2 188.6 %all-to-all-start = ((bf16[64,64,1024]{2,1,0:T(8,128)(2,1)}), bf16[64,64,1024]{2,1,0:T(8,128)(2,1)}, u32[]{:S(2)}, u32[]{:S(2)}) async-start(bf16[64,64,1024]{2,1,0:T(8,128)(2,1)} %bitcast.21), calls=%async_computation | async-start | bytes 16777216 | tf_op jit(solution)/shard_map/all_to_all | solution.py:50
  47.2 282.5 %reduce-scatter.2.cloned.1.call-start = ((), (), s32[]{:S(2)}) async-start(), calls=%async_computation.4 | async-start | bytes 5242880 | tf_op jit(solution)/shard_map/reduce_scatter | solution.py:59
  264.9 52.4 %all-to-all-start.1 = ((bf16[8,512,256]{2,0,1:T(8,128)(2,1)}), bf16[8,512,256]{2,0,1:T(8,128)(2,1)S(1)}, u32[]{:S(2)}, u32[]{:S(2)}) async-start(bf16[8,512,256]{2,0,1:T(8,128)(2,1)} %copy.18), calls=%async_computation.1 | async-start | bytes 4194304 | tf_op jit(solution)/shard_map/all_to_all | solution.py:57
  317.3 1.3 copy-start
Sparse Core Ops, SparseCore 0:
  246.1 43.6 reduce-scatter.1
where the time goes:
time: 340 us
  waiting for transfers between devices  221 us (65%)
  local copies, waits for them, and re-layouts  48.4 us (14%)
  starting transfers between devices  17.5 us (5%)
  matrix products  17.4 us (5%)
  between operations  14.1 us (4%)
  other arithmetic  13.4 us (4%)
  blocking collectives  7.71 us (2%)
    all_to_all x1, waiting for transfers between devices, shards(): lax.all_to_all(outgoing, 'dev', split_axis=0, concat_axis=1, tiled=True)  181 us
    all_to_all x1, waiting for transfers between devices, shards(): lax.all_to_all(dists, 'dev', split_axis=1, concat_axis=0, tiled=True)  40.2 us
    scatter x1, local copies, waits for them, and re-layouts, shards(): jnp.zeros((nblocks * depth, width), jnp.bfloat16).at[slots].set(points)  15.2 us
    gather x1, local copies, waits for them, and re-layouts, shards(): distances = returned.reshape(nblocks * depth, block_size)[slots]  9.06 us
    all_to_all x1, local copies, waits for them, and re-layouts, shards(): lax.all_to_all(outgoing, 'dev', split_axis=0, concat_axis=1, tiled=True)  8.39 us
    scatter x1, local copies, waits for them, and re-layouts, shards(): targets = jnp.full((nblocks * depth,), -1, jnp.int32).at[slots].set(finals)  8.23 us
    psum x1, blocking collectives, shards(): all_counts = lax.psum(counts, 'grp')  7.71 us
    dot_general x1, matrix products, block_work(): jnp.einsum('xnt,xni->xti', onehot_assign.astype(jnp.bfloat16), received_p...  7.67 us
  transfers between devices with their start and end apart: 4, of which 2 were waited for; matrix products, arithmetic and copies ran while one was open for 14% of the time, Pallas kernels for 0%

commit v1 on v0

--- a/solution.py
+++ b/solution.py
@@ -4,6 +4,13 @@
 from jax.sharding import PartitionSpec as P
 
 BS = 256
+
+
+def remake_sections(xx):
+    found_now = jnp.concatenate(
+        lax.all_to_all(jnp.stack(jnp.split(xx, lax.axis_size("dev"), axis=0)), "dev", 0, 0), 1
+    )
+    return found_now
 
 
 def block_work(received_points, wanted, centroid_table, width, block_size):
@@ -47,7 +54,7 @@
     outgoing = outgoing.reshape(nblocks, depth, width)
     targets = targets.reshape(nblocks, depth)
     received_points, wanted = (
-        lax.all_to_all(outgoing, "dev", split_axis=0, concat_axis=1, tiled=True),
+        remake_sections(outgoing),
         lax.all_to_all(targets, "dev", split_axis=0, concat_axis=1, tiled=True),
     )
     centroid_table = centroids.reshape(owned, block_size, width)

time: 340 us -> 354 us (1.041)
  local copies, waits for them, and re-layouts: 48.4 us -> 60.8 us
    all_to_all x1 -> x0, local copies, waits for them, and re-layouts: 8.39 us -> none  [shards(): lax.all_to_all(outgoing, 'dev', split_axis=0, concat_axis=1, tiled=True)]
    reshape x0 -> x1, local copies, waits for them, and re-layouts: none -> 8.39 us  [remake_sections(): jnp.concatenate(lax.all_to_all(jnp.stack(jnp.split(xx, lax.axis_size('dev...]
    unnamed x7 -> x12, local copies, waits for them, and re-layouts: 2.1 us -> 9.56 us
    split x0 -> x1, local copies, waits for them, and re-layouts: none -> 3.89 us  [remake_sections(): jnp.split(xx, lax.axis_size('dev'), axis=0)]
  transfers between devices with their start and end apart: 4 -> 4, of which waited for: 2 -> 2; matrix products, arithmetic and copies ran while one was open for 14% -> 17% of each run, Pallas kernels for 0% -> 0%
where the time goes in v1:
time: 354 us; the launch traced here: 353 us
  waiting for transfers between devices  221 us (62%)
  local copies, waits for them, and re-layouts  60.8 us (17%)
  starting transfers between devices  17.5 us (5%)
  matrix products  17.4 us (5%)
  other arithmetic  14.1 us (4%)
  between operations  14.1 us (4%)
  blocking collectives  7.71 us (2%)
    all_to_all x1, waiting for transfers between devices, remake_sections(): lax.all_to_all(jnp.stack(jnp.split(xx, lax.axis_size('dev'), axis=0)), 'd...  181 us
    all_to_all x1, waiting for transfers between devices, shards(): lax.all_to_all(dists, 'dev', split_axis=1, concat_axis=0, tiled=True)  40.2 us
    scatter x1, local copies, waits for them, and re-layouts, shards(): jnp.zeros((nblocks * depth, width), jnp.bfloat16).at[slots].set(points)  15.3 us
    unnamed x12, local copies, waits for them, and re-layouts  9.56 us
    gather x1, local copies, waits for them, and re-layouts, shards(): distances = returned.reshape(nblocks * depth, block_size)[slots]  9.06 us
    reshape x1, local copies, waits for them, and re-layouts, remake_sections(): jnp.concatenate(lax.all_to_all(jnp.stack(jnp.split(xx, lax.axis_size('dev...  8.39 us
    scatter x1, local copies, waits for them, and re-layouts, shards(): targets = jnp.full((nblocks * depth,), -1, jnp.int32).at[slots].set(finals)  8.23 us
    psum x1, blocking collectives, shards(): all_counts = lax.psum(counts, 'grp')  7.71 us
  transfers between devices with their start and end apart: 4, of which 2 were waited for; matrix products, arithmetic and copies ran while one was open for 17% of the time, Pallas kernels for 0%

profile of v1, /device:TPU:0, one launch (start us, length us, event | category | flops | bytes accessed | tf_op | source)
XLA Modules:
  0.0 352.9 jit_solution(4652592949994320993)
XLA Ops:
  7.2 2.4 fusion.7
  9.6 0.7 compare_select_fusion
  10.3 8.2 %scatter_custom_fusion.1 = s32[4096]{0:T(1024)S(1)} fusion(s32[2048]{0:T(1024)S(1)} %bitcast.41, s32[2048]{0:T(1024)} %param.6, s32[]{:T(128)} %constant.8.clone.1), kind=kCustom, calls=%fused_computation.29 | custom fusion | bytes 16896 | tf_op jit(solution)/shard_map/scatter | solution.py:53
  18.6 0.1 all_to_all.30
  18.6 0.7 reshape.94
  19.3 7.3 %all-to-all-start.2 = ((s32[8,1,512]{2,1,0:T(1,128)}), s32[8,1,512]{2,1,0:T(1,128)S(1)}, u32[]{:S(2)}, u32[]{:S(2)}) async-start(s32[8,1,512]{2,1,0:T(1,128)} %reshape.94), calls=%async_computation.2 | async-start | bytes 32768 | tf_op jit(solution)/shard_map/all_to_all | solution.py:58
  26.6 15.3 %scatter_custom_fusion = bf16[4096,1024]{1,0:T(8,128)(2,1)} fusion(s32[2048]{0:T(1024)S(1)} %bitcast.42, bf16[2048,1024]{1,0:T(8,128)(2,1)} %param.4, bf16[]{:T(256)} %constant.12.clone.1), kind=kCustom, calls=%fused_computation.11 | custom fusion | bytes 8389120 | tf_op jit(solution)/shard_map/scatter | solution.py:52
  41.9 3.9 %fusion.11 = (bf16[512,1024]{1,0:T(8,128)(2,1)S(1)}, bf16[512,1024]{1,0:T(8,128)(2,1)S(1)}, bf16[512,1024]{1,0:T(8,128)(2,1)S(1)}, bf16[512,1024]{1,0:T(8,128)(2...) fusion(bf16[4096,1024]{1,0:T(8,128)(2,1)} %scatter_custom_fusion), kind=kLoop, calls=%fused_computation.33 | loop fusion | bytes 16777216 | tf_op jit(solution)/shard_map/split | solution.py:11
  45.8 1.1 constant_dynamic-update-slice_fusion.7
  46.9 1.0 constant_dynamic-update-slice_fusion.6
  48.0 1.0 constant_dynamic-update-slice_fusion.5
  49.0 1.0 constant_dynamic-update-slice_fusion.4
  50.1 1.1 constant_dynamic-update-slice_fusion.3
  51.2 1.0 constant_dynamic-update-slice_fusion.2
  52.2 1.0 constant_dynamic-update-slice_fusion.1
  53.3 1.1 constant_dynamic-update-slice_fusion
  54.3 0.0 all-to-all-done.2
  54.3 6.0 %all-to-all-start = ((bf16[8,8,64,1024]{3,2,1,0:T(8,128)(2,1)}), bf16[8,8,64,1024]{3,2,1,0:T(8,128)(2,1)}, u32[]{:S(2)}, u32[]{:S(2)}) async-start(bf16[8,8,64,1024]{3,2,1,0:T(8,128)(2,1)} %constant_dynamic-update-slice_fusion), calls=%async_computation | async-start | bytes 16777216 | tf_op jit(solution)/shard_map/all_to_all | solution.py:11
  60.3 0.2 reduce-scatter.2.cloned.1.call-start
  60.6 0.5 broadcast.19
  61.1 0.7 reduce.2
  61.8 0.1 reshape.95
  61.9 0.1 eq.34
  61.9 181.0 %all-to-all-done = bf16[8,8,64,1024]{3,2,1,0:T(8,128)(2,1)} async-done(((bf16[8,8,64,1024]{3,2,1,0:T(8,128)(2,1)}), bf16[8,8,64,1024]{3,2,1,0:T(8,128)(2,1)}, u32[]{:S(2)}, u32[]{:S(2)}) %all-to-all-start) | async-done | bytes 8388640 | tf_op jit(solution)/shard_map/all_to_all | solution.py:11
  242.9 8.4 %copy.35 = bf16[8,8,64,1024]{3,2,1,0:T(8,128)(2,1)} copy(bf16[8,8,64,1024]{3,2,0,1:T(8,128)(2,1)} %bitcast.11) | data formatting | bytes 16777216 | tf_op jit(solution)/shard_map/reshape | solution.py:10
  251.3 7.7 %fusion.4 = bf16[8,256,1024]{2,1,0:T(8,128)(2,1)} fusion(bf16[8,512,1024]{2,1,0:T(8,128)(2,1)} %bitcast.27, s32[8,512]{1,0:T(8,128)S(1)} %eq.34), kind=kOutput, calls=%fused_computation.13 | convolution fusion | flops 2150629376 | bytes 12599296 | tf_op jit(solution)/shard_map/xnt,xni->xti/dot_general | solution.py:26
  259.0 0.0 reduce-scatter.2.cloned.1.call-update
  259.0 3.1 multiply_reduce_fusion.1
  262.1 6.0 %multiply_reduce_fusion = f32[8,8,64]{2,0,1:T(8,128)S(1)} fusion(bf16[8,8,64,1024]{3,2,1,0:T(8,128)(2,1)} %all-to-all-done), kind=kLoop, calls=%fused_computation.3 | loop fusion | flops 12578816 | bytes 8404992 | tf_op jit(solution)/shard_map/reduce_sum | solution.py:18
  268.1 0.1 sub.10
  268.2 7.3 %multiply_convert_fusion = bf16[8,512,256]{2,1,0:T(8,128)(2,1)S(1)} fusion(bf16[8,512,1024]{2,1,0:T(8,128)(2,1)} %bitcast.28, bf16[8,256,1024]{2,1,0:T(8,128)(2,1)} %bitcast.30, f32[8,256]{1,0:T(8,128)S(1)} %add.38, f32[8,512]{1,0:T(8,128)S(1)} %sub.10), kind=kOutput, calls=%fused_computation.10 | convolution fusion | flops 2152726528 | bytes 14704640 | tf_op jit(solution)/shard_map/nzy,nvy->nzv/dot_general | solution.py:19
  275.5 2.5 copy.36
  278.0 3.9 %all-to-all-start.1 = ((bf16[8,512,256]{2,0,1:T(8,128)(2,1)}), bf16[8,512,256]{2,0,1:T(8,128)(2,1)S(1)}, u32[]{:S(2)}, u32[]{:S(2)}) async-start(bf16[8,512,256]{2,0,1:T(8,128)(2,1)} %copy.36), calls=%async_computation.1 | async-start | bytes 4194304 | tf_op jit(solution)/shard_map/all_to_all | solution.py:64
  281.9 0.5 convert_reduce_fusion
  282.4 7.7 %psum.7 = f32[2048]{0:T(1024)S(1)} all-reduce(f32[2048]{0:T(1024)S(1)} %bitcast.46), channel_id=1, replica_groups=mesh['grp'=4,'dev'=8] {'grp'}, use_global_device_ids=true, to_apply=%region_7.8 | all-reduce | flops 2048 | bytes 16384 | tf_op jit(solution)/shard_map/psum | solution.py:69
  290.2 40.2 %all-to-all-done.1 = bf16[8,512,256]{2,0,1:T(8,128)(2,1)S(1)} async-done(((bf16[8,512,256]{2,0,1:T(8,128)(2,1)}), bf16[8,512,256]{2,0,1:T(8,128)(2,1)S(1)}, u32[]{:S(2)}, u32[]{:S(2)}) %all-to-all-start.1) | async-done | bytes 2097184 | tf_op jit(solution)/shard_map/all_to_all | solution.py:64
  330.4 0.0 copy-start
  330.4 1.3 copy-done
  331.7 2.1 copy.37
  333.8 9.1 %gather_fusion = bf16[2048,256]{1,0:T(8,128)(2,1)} fusion(bf16[4096,256]{1,0:T(8,128)(2,1)S(1)} %bitcast.26, s32[2048]{0:T(1024)S(1)} %broadcast_clamp_fusion), kind=kCustom, calls=%fused_computation | custom fusion | bytes 2105344 | tf_op jit(solution)/shard_map/gather | solution.py:65
  342.9 0.0 reduce-scatter.2.cloned.1.call-done
  342.9 3.2 add_divide_fusion
  (7 shorter events, 0.0 us)
Async XLA Ops:
  19.3 35.0 %all-to-all-start.2 = ((s32[8,1,512]{2,1,0:T(1,128)}), s32[8,1,512]{2,1,0:T(1,128)S(1)}, u32[]{:S(2)}, u32[]{:S(2)}) async-start(s32[8,1,512]{2,1,0:T(1,128)} %reshape.94), calls=%async_computation.2 | async-start | bytes 32768 | tf_op jit(solution)/shard_map/all_to_all | solution.py:58
  54.3 188.6 %all-to-all-start = ((bf16[8,8,64,1024]{3,2,1,0:T(8,128)(2,1)}), bf16[8,8,64,1024]{3,2,1,0:T(8,128)(2,1)}, u32[]{:S(2)}, u32[]{:S(2)}) async-start(bf16[8,8,64,1024]{3,2,1,0:T(8,128)(2,1)} %constant_dynamic-update-slice_fusion), calls=%async_computation | async-start | bytes 16777216 | tf_op jit(solution)/shard_map/all_to_all | solution.py:11
  60.3 282.5 %reduce-scatter.2.cloned.1.call-start = ((), (), s32[]{:S(2)}) async-start(), calls=%async_computation.4 | async-start | bytes 5242880 | tf_op jit(solution)/shard_map/reduce_scatter | solution.py:66
  278.0 52.4 %all-to-all-start.1 = ((bf16[8,512,256]{2,0,1:T(8,128)(2,1)}), bf16[8,512,256]{2,0,1:T(8,128)(2,1)S(1)}, u32[]{:S(2)}, u32[]{:S(2)}) async-start(bf16[8,512,256]{2,0,1:T(8,128)(2,1)} %copy.36), calls=%async_computation.1 | async-start | bytes 4194304 | tf_op jit(solution)/shard_map/all_to_all | solution.py:64
  330.4 1.3 copy-start
Sparse Core Ops, SparseCore 0:
  259.1 43.7 reduce-scatter.1
